TPU v7x, 256 devices: a whole 4x4x8 slice. The times are simulated.
256 devices in a mesh: grp: 8 (over y, core), dom: 32 (over z, x).
Axes of the slice: x: 4, y: 4, z: 8, core: 2. Of those that a mesh axis runs over, the one named last changes fastest.
Arguments:
- element_state: float32 [56, 9, 163840], P(None, None, ('grp', 'dom')), may hold values from -6 to 6
- stiffness: float32 [3, 56, 56], replicated, may hold values from -0.75 to 0.75
- flux_local: float32 [4, 56, 56], replicated, may hold values from -0.75 to 0.75
- flux_remote: float32 [4, 56, 56], replicated, may hold values from -0.75 to 0.75
- star_matrix: float32 [3, 9, 9, 163840], P(None, None, None, ('grp', 'dom')), may hold values from -0.18 to 0.18
- face_local: float32 [4, 9, 9, 163840], P(None, None, None, ('grp', 'dom')), may hold values from -0.15 to 0.15
- face_remote: float32 [4, 9, 9, 163840], P(None, None, None, ('grp', 'dom')), may hold values from -0.15 to 0.15
- energy_weight: float32 [9, 163840], P(None, ('grp', 'dom')), may hold values from 0.5 to 18
- face_neighbour: int32 [4, 163840], P(None, ('grp', 'dom')), may hold values from 0 to 1151, as said below
- element_count: int32 [256], P(('grp', 'dom')), may hold values from 160 to 640, as said below
- send_count: int32 [256, 8], P(('grp', 'dom')), may hold values from 0 to 64, as said below
- send_element: int32 [256, 8, 64], P(('grp', 'dom')), may hold values from 0 to 639, as said below
- receiver_element: int32 [4096], P(('grp', 'dom')), may hold values from 0 to 639, as said below
- receiver_slot: int32 [4096], P(('grp', 'dom')), may hold values from 0 to 511, as said below
- receiver_weight: float32 [56, 4096], P(None, ('grp', 'dom')), may hold values from -0.75 to 0.75
Outputs:
- new_state: float32 [56, 9, 163840], P(None, None, ('grp', 'dom'))
- energy: float32 [8, 3], P('grp')
- traces: float32 [3, 9, 4096], P(None, None, ('grp', 'dom'))
Inputs may be any that keep to these rules, and one draw needn't show every extreme that they name: The first element_count[p] slots of a partition are active. In every slab 4 partitions in a row along dom (cyclically) hold 640 active elements; the others hold from 160 to 320. `send_count`: every partition has exactly 64 in one of its first 6 slots. `send_element`: names active elements of the sending partition. `face_neighbour`: values below 640 name active elements of the partition itself. `receiver_element`: names an active element of the owning partition. `receiver_slot`: within each slab a permutation of the 512 rows.
All inputs are finite; a program needn't handle non-finite values.
Results may differ from a plain program's by a relative error of at most 0.0001.
Values sent between devices are 32-bit elements; how exact they have to be, the bound alone decides.
A program may use at most 128 MiB of HBM per device.

v0:
```python
import jax
import jax.numpy as jnp
from jax import lax
from jax.experimental import pallas as pl
from jax.experimental.pallas import tpu as pltpu
from jax.sharding import PartitionSpec as P

STEPS = 3
REACH = 3
GRP_DOM = ("grp", "dom")
MESH = pl.DeviceIdType.MESH
f32 = jnp.float32
bf16 = jnp.bfloat16
highest = lax.Precision.HIGHEST
LANES = 128
CHUNKS = 4
ROWS_LHS = 176
TN = (((0,), (0,)), ((), ()))
NT = (((1,), (1,)), ((), ()))


def offset_of(slot):
    return slot + 1 if slot < REACH else REACH - 1 - slot


def split(value):
    hi = value.astype(bf16)
    return hi, (value - hi.astype(f32)).astype(bf16)


def lane_block(number):
    return pl.ds(pl.multiple_of(number * LANES, LANES), LANES)


def make_kernel(groups, places, elems, cap):
    slots = 2 * REACH + 2
    blocks = elems // LANES
    sent = slots * cap
    receivers = 16

    def kernel(
        state_ref, stiff_ref, flux_ref, fluxr_ref, star_ref, face_ref, facer_ref,
        weight_ref, live_ref, number_ref, recw_ref,
        x_ref, energy_ref, trace_ref,
        y_ref, v_ref, part_ref, xt_ref, send_buf, halo_ref, hb_ref, own_ref, nb_ref, vr_ref,
        pick_ref, pack_ref, af_ref, a_ref, rf_ref, ra_ref, rb_ref,
        en_ref, rec_ref, table_ref, msg_ref, all_ref,
        send_sem, recv_sem, last_send, last_recv,
    ):
        g = lax.axis_index("grp")
        d = lax.axis_index("dom")

        for t in range(STEPS):
            halo_ref[t, 2 * REACH * cap :, :] = jnp.zeros((2 * cap, CHUNKS * LANES), f32)
        barrier = pltpu.get_barrier_semaphore()

        def greet(k, carry):
            peer = lax.rem(d + k, places)
            pl.semaphore_signal(barrier, inc=1, device_id=(g, peer), device_id_type=MESH)
            return carry

        lax.fori_loop(1, places, greet, 0)

        @pl.when(g < groups - 1)
        def _():
            pl.semaphore_signal(barrier, inc=1, device_id=(g + 1, d), device_id_type=MESH)

        @pl.when(g > 0)
        def _():
            pl.semaphore_signal(barrier, inc=1, device_id=(g - 1, d), device_id_type=MESH)

        for q in range(9):
            x_ref[q] = state_ref[q]

        lane = lax.broadcasted_iota(jnp.int32, (LANES, LANES), 1).astype(f32)

        def column(number):
            return jnp.broadcast_to(number_ref[number], (LANES, LANES)).T

        def hot(names, tile):
            return jnp.maximum(1.0 - jnp.abs(names - (lane + float(tile * LANES))), 0.0).astype(bf16)

        def pack_rows(i, carry):
            names = column(4 * blocks + i)
            at = pl.ds(pl.multiple_of(i * LANES, LANES), LANES)
            for tile in range(blocks):
                pack_ref[at, tile * LANES : (tile + 1) * LANES] = hot(names, tile)
            return carry

        lax.fori_loop(0, sent // LANES + 1, pack_rows, 0)

        def to_rows():
            def body(block, carry):
                at = lane_block(block)
                for j in range(CHUNKS):
                    size = min(16, 56 - 16 * j)
                    pieces = [x_ref[2 * j, :, at], x_ref[2 * j + 1, :, at], x_ref[8, pl.ds(16 * j, size), at]]
                    if size < 16:
                        pieces.append(jnp.zeros((16 - size, LANES), f32))
                    hi, lo = split(jnp.concatenate(pieces, axis=0).T)
                    xt_ref[at, 2 * j * LANES : (2 * j + 1) * LANES] = hi
                    xt_ref[at, (2 * j + 1) * LANES : (2 * j + 2) * LANES] = lo
                return carry

            lax.fori_loop(0, blocks, body, 0)

        def pack(first, count):
            for j in range(CHUNKS):
                taken = jnp.dot(
                    pack_ref[first : first + count, :],
                    xt_ref[:, 2 * j * LANES : (2 * j + 2) * LANES],
                    preferred_element_type=f32,
                )
                whole = taken[:, :LANES] + taken[:, LANES:]
                if first == 0:
                    send_buf[:, j * LANES : (j + 1) * LANES] = whole[:sent]
                    rec_ref[:, j * LANES : (j + 1) * LANES] = whole[sent:]
                else:
                    rec_ref[:, j * LANES : (j + 1) * LANES] = whole

        def copies(t):
            made = []
            for slot in range(slots):
                if slot < 2 * REACH:
                    target = (g, lax.rem(d + offset_of(slot) + places, places))
                else:
                    target = (g + (1 if slot == 2 * REACH else -1), d)
                made.append(
                    pltpu.make_async_remote_copy(
                        src_ref=send_buf.at[pl.ds(slot * cap, cap)],
                        dst_ref=halo_ref.at[t, pl.ds(slot * cap, cap)],
                        send_sem=send_sem.at[slot],
                        recv_sem=recv_sem.at[t, slot],
                        device_id=target,
                        device_id_type=MESH,
                    )
                )
            return made

        def trace(t):
            at = lax.broadcasted_iota(jnp.int32, (CHUNKS * LANES, LANES), 0)
            inside = at % LANES
            quantity = jnp.where(inside < 56, at // LANES * 2, jnp.where(inside < 112, at // LANES * 2 + 1, 8))
            out = lax.broadcasted_iota(jnp.int32, (CHUNKS * LANES, LANES), 1)
            placed = jnp.where(out == 9 * t + quantity, 1.0, 0.0).astype(f32)
            table_ref[...] += jnp.dot(
                rec_ref[...] * recw_ref[...], placed, precision=highest, preferred_element_type=f32
            )

        to_rows()
        table_ref[...] = jnp.zeros_like(table_ref)
        en_ref[...] = jnp.zeros_like(en_ref)

        def step(t, carry):
            pack(0, sent + receivers)

            @pl.when(t == 0)
            def _():
                waits = places - 1 + jnp.where(g > 0, 1, 0) + jnp.where(g < groups - 1, 1, 0)
                pl.semaphore_wait(barrier, waits)

            moves = copies(t)
            for slot in range(2 * REACH):
                moves[slot].start()

            @pl.when(g < groups - 1)
            def _():
                moves[6].start()

            @pl.when(g > 0)
            def _():
                moves[7].start()

            @pl.when(t == 0)
            def _():
                af_ref[...] = jnp.zeros_like(af_ref)
                for m in range(7):
                    matrix = stiff_ref[m] if m < 3 else -flux_ref[m - 3]
                    for part in range(4):
                        af_ref[pl.ds(56 * m, 56), pl.ds(64 * part, 56)] = matrix
                whole = af_ref[...]
                rounded = whole.astype(bf16).astype(f32)
                part = lax.broadcasted_iota(jnp.int32, whole.shape, 1) // 64
                a_ref[...] = jnp.where(part % 2 == 0, rounded, whole - rounded).astype(bf16)
                for f in range(4):
                    matrix = -fluxr_ref[f]
                    for j in range(CHUNKS):
                        rf_ref[...] = jnp.zeros_like(rf_ref)
                        rf_ref[pl.ds(0, 56), pl.ds(0, 56)] = matrix
                        rf_ref[pl.ds(56, 56), pl.ds(56, 56)] = matrix
                        size = min(16, 56 - 16 * j)
                        rf_ref[pl.ds(112, 56), pl.ds(112, size)] = matrix[:, 16 * j : 16 * j + size]
                        hi, lo = split(rf_ref[...])
                        ra_ref[f, j] = jnp.concatenate([hi, hi], axis=1)
                        rb_ref[f, j] = jnp.concatenate([lo, lo], axis=1)

                def face_rows(i, carry):
                    names = column(i)
                    f = i // blocks
                    at = pl.ds(pl.multiple_of(i % blocks * LANES, LANES), LANES)
                    for tile in range(blocks + sent // LANES):
                        pick_ref[f, at, tile * LANES : (tile + 1) * LANES] = hot(names, tile)
                    return carry

                lax.fori_loop(0, 4 * blocks, face_rows, 0)

            @pl.when(t > 0)
            def _():
                trace(t - 1)

            def modal(q, carry):
                pad = jnp.zeros((8, elems), f32)
                value = jnp.concatenate([x_ref[q], pad], axis=0)
                hi, lo = split(value)
                y_ref[0:64, :] = hi
                y_ref[64:128, :] = hi
                y_ref[128:192, :] = lo
                y_ref[192:256, :] = lo
                v_ref[q] = jnp.dot(a_ref[...], y_ref[...], preferred_element_type=f32)
                return carry

            lax.fori_loop(0, 9, modal, 0)

            def local_map(number, carry):
                block = number // 3
                first = (number % 3) * 3
                at = lane_block(block)
                total = [jnp.zeros((56, LANES), f32) for _ in range(3)]
                for m in range(7):
                    maps, n = (star_ref, m) if m < 3 else (face_ref, m - 3)
                    for q in range(9):
                        term = v_ref[q, pl.ds(56 * m, 56), at]
                        for i in range(3):
                            total[i] = total[i] + maps[first + i, q, pl.ds(n, 1), at] * term
                for i in range(3):
                    part_ref[first + i, :, at] = total[i]
                return carry

            lax.fori_loop(0, blocks * 3, local_map, 0)

            def own(f, carry):
                for j in range(CHUNKS):
                    own_ref[f, j] = jnp.dot(
                        pick_ref[f, :, :elems],
                        xt_ref[:, 2 * j * LANES : (2 * j + 2) * LANES],
                        preferred_element_type=f32,
                    ).astype(bf16)
                return carry

            lax.fori_loop(0, 4, own, 0)

            for slot in range(2 * REACH):
                moves[slot].wait_recv()

            @pl.when(g > 0)
            def _():
                moves[6].wait_recv()

            @pl.when(g < groups - 1)
            def _():
                moves[7].wait_recv()

            for j in range(CHUNKS):
                hi, lo = split(halo_ref[t, :, j * LANES : (j + 1) * LANES])
                hb_ref[:, 2 * j * LANES : (2 * j + 1) * LANES] = hi
                hb_ref[:, (2 * j + 1) * LANES : (2 * j + 2) * LANES] = lo

            def remote(f, carry):
                for j in range(CHUNKS):
                    far = jnp.dot(
                        pick_ref[f, :, elems:],
                        hb_ref[:, 2 * j * LANES : (2 * j + 2) * LANES],
                        preferred_element_type=f32,
                    ).astype(bf16)
                    nb_ref[...] = own_ref[f, j] + far
                    near = nb_ref[...]
                    both = lax.dot_general(ra_ref[f, j], near, NT, preferred_element_type=f32)
                    both = both + lax.dot_general(rb_ref[f, j], near, NT, preferred_element_type=f32)
                    vr_ref[f, 2 * j] = both[0:56]
                    vr_ref[f, 2 * j + 1] = both[56:112]
                    if j == 0:
                        vr_ref[f, 8] = both[112:168]
                    else:
                        vr_ref[f, 8] += both[112:168]
                return carry

            lax.fori_loop(0, 4, remote, 0)

            def remote_map(number, energy):
                block = number // 3
                first = (number % 3) * 3
                at = lane_block(block)
                live = live_ref[0, :, at]
                total = [part_ref[first + i, :, at] for i in range(3)]
                for f in range(4):
                    for q in range(9):
                        term = vr_ref[f, q, :, at]
                        for i in range(3):
                            total[i] = total[i] + facer_ref[first + i, q, pl.ds(f, 1), at] * term
                for i in range(3):
                    new = x_ref[first + i, :, at] + live * total[i]
                    x_ref[first + i, :, at] = new
                    squares = jnp.sum(new * new, axis=0, keepdims=True)
                    energy = energy + weight_ref[first + i, :, at] * squares
                return energy

            energy = lax.fori_loop(0, blocks * 3, remote_map, jnp.zeros((1, LANES), f32))
            sub = lax.broadcasted_iota(jnp.int32, (8, LANES), 0)
            en_ref[...] += jnp.where(sub == t, energy, 0.0)
            to_rows()

            for slot in range(2 * REACH):
                moves[slot].wait_send()

            @pl.when(g < groups - 1)
            def _():
                moves[6].wait_send()

            @pl.when(g > 0)
            def _():
                moves[7].wait_send()

            return carry

        lax.fori_loop(0, STEPS, step, 0)
        pack(sent, receivers)
        trace(STEPS - 1)

        row = lax.broadcasted_iota(jnp.int32, (receivers, LANES), 0)
        col = lax.broadcasted_iota(jnp.int32, (receivers, LANES), 1)
        rows = column(4 * blocks + sent // LANES + 1)[:receivers]
        sums = jnp.sum(en_ref[...], axis=1, keepdims=True)
        table = table_ref[...] + jnp.where(col == 27, rows, 0.0)
        for t in range(STEPS):
            table = table + jnp.where((col == 28 + t) & (row == 0), sums[t : t + 1], 0.0)
        half = receivers // 2
        msg_ref[...] = table[:half] + pltpu.roll(table[half:], 64, 1)

        def last(k):
            return pltpu.make_async_remote_copy(
                src_ref=msg_ref,
                dst_ref=all_ref.at[d],
                send_sem=last_send.at[k],
                recv_sem=last_recv.at[k],
                device_id=(g, lax.rem(d + k, places)),
                device_id_type=MESH,
            )

        def arrival(k):
            return pltpu.make_async_remote_copy(
                src_ref=msg_ref,
                dst_ref=all_ref.at[lax.rem(d + places - k, places)],
                send_sem=last_send.at[k],
                recv_sem=last_recv.at[k],
                device_id=(g, lax.rem(d + k, places)),
                device_id_type=MESH,
            )

        def start_last(k, carry):
            last(k).start()
            return carry

        def end_last(k, carry):
            arrival(k).wait_recv()
            last(k).wait_send()
            return carry

        lax.fori_loop(1, places, start_last, 0)
        all_ref[d] = msg_ref[...]
        lax.fori_loop(1, places, end_last, 0)

        arrived = all_ref[...].reshape(places * half, LANES)
        energy_ref[...] = jnp.broadcast_to(jnp.sum(arrived, axis=0, keepdims=True), energy_ref.shape)
        mine = lax.broadcasted_iota(jnp.int32, (places * half, LANES), 1).astype(f32)
        mine = mine + (d * receivers).astype(f32)
        keep = lax.broadcasted_iota(jnp.int32, (places * half, LANES), 1) < receivers
        result = jnp.zeros(trace_ref.shape, f32)
        for part in range(2):
            names = jnp.broadcast_to(arrived[:, 64 * part + 27 : 64 * part + 28], (places * half, LANES))
            chosen = jnp.maximum(1.0 - jnp.abs(names - mine), 0.0)
            chosen = jnp.where(keep, chosen, 0.0)
            picked = lax.dot_general(arrived, chosen, TN, precision=highest, preferred_element_type=f32)
            result = result + picked[64 * part : 64 * part + 32]
        trace_ref[...] = result

    return kernel


def per_device(groups, places):
    def run(
        element_state, stiffness, flux_local, flux_remote, star_matrix, face_local, face_remote,
        energy_weight, face_neighbour, element_count, send_count, send_element,
        receiver_element, receiver_slot, receiver_weight,
    ):
        basis, quantities, elems = element_state.shape
        slots, cap = send_element.shape[1:]
        sent = slots * cap
        receivers = receiver_slot.shape[0]
        turned = receiver_weight.T
        tail = jnp.pad(turned, ((0, 0), (0, 8))).reshape(receivers, CHUNKS, 16)
        pair = jnp.broadcast_to(turned[:, None, :], (receivers, CHUNKS, basis))
        recw = jnp.concatenate([pair, pair, tail], axis=2).reshape(receivers, CHUNKS * LANES)
        live = (jnp.arange(elems) < element_count[0]).astype(f32)
        weight = (energy_weight * live[None])[:, None, :]
        filled = jnp.arange(cap)[None, :] < send_count[0][:, None]
        wanted = jnp.where(filled, send_element[0], -1)
        fill = LANES - receivers
        numbers = jnp.concatenate(
            [
                face_neighbour.reshape(-1, LANES),
                wanted.reshape(-1, LANES),
                jnp.pad(receiver_element, (0, fill), constant_values=-1)[None],
                jnp.pad(receiver_slot, (0, fill), constant_values=-1)[None],
            ],
            axis=0,
        ).astype(f32)[:, None, :]

        vmem = pl.BlockSpec(memory_space=pltpu.VMEM)
        wide = CHUNKS * LANES
        faces = 4
        state, energy, table = pl.pallas_call(
            make_kernel(groups, places, elems, cap),
            out_shape=(
                jax.ShapeDtypeStruct((quantities, basis, elems), f32),
                jax.ShapeDtypeStruct((8, LANES), f32),
                jax.ShapeDtypeStruct((32, LANES), f32),
            ),
            in_specs=[vmem] * 11,
            out_specs=(vmem, vmem, vmem),
            scratch_shapes=[
                pltpu.VMEM((256, elems), bf16),
                pltpu.VMEM((9, 400, elems), f32),
                pltpu.VMEM((9, 56, elems), f32),
                pltpu.VMEM((elems, 2 * wide), bf16),
                pltpu.VMEM((sent, wide), f32),
                pltpu.VMEM((STEPS, sent, wide), f32),
                pltpu.VMEM((sent, 2 * wide), bf16),
                pltpu.VMEM((faces, CHUNKS, elems, 2 * LANES), bf16),
                pltpu.VMEM((elems, 2 * LANES), bf16),
                pltpu.VMEM((faces, 9, 56, elems), f32),
                pltpu.VMEM((faces, elems, elems + sent), bf16),
                pltpu.VMEM((sent + LANES, elems), bf16),
                pltpu.VMEM((400, 256), f32),
                pltpu.VMEM((400, 256), bf16),
                pltpu.VMEM((ROWS_LHS, LANES), f32),
                pltpu.VMEM((faces, CHUNKS, ROWS_LHS, 2 * LANES), bf16),
                pltpu.VMEM((faces, CHUNKS, ROWS_LHS, 2 * LANES), bf16),
                pltpu.VMEM((8, LANES), f32),
                pltpu.VMEM((receivers, wide), f32),
                pltpu.VMEM((receivers, LANES), f32),
                pltpu.VMEM((receivers // 2, LANES), f32),
                pltpu.VMEM((places, receivers // 2, LANES), f32),
                pltpu.SemaphoreType.DMA((slots,)),
                pltpu.SemaphoreType.DMA((STEPS, slots)),
                pltpu.SemaphoreType.DMA((places,)),
                pltpu.SemaphoreType.DMA((places,)),
            ],
            compiler_params=pltpu.CompilerParams(
                collective_id=0, has_side_effects=True, vmem_limit_bytes=60 * 1024 * 1024
            ),
        )(
            element_state.transpose(1, 0, 2), stiffness, flux_local, flux_remote,
            star_matrix.transpose(1, 2, 0, 3), face_local.transpose(1, 2, 0, 3),
            face_remote.transpose(1, 2, 0, 3),
            weight, live[None, None], numbers, recw,
        )
        total = energy[:1, 28 : 28 + STEPS] * 0.5 / float(places * elems * basis * quantities)
        traces = table[: STEPS * quantities, :receivers].reshape(STEPS, quantities, receivers)
        return state.transpose(1, 0, 2), total, traces

    return run


def solution(mesh):
    return jax.shard_map(
        per_device(mesh.shape["grp"], mesh.shape["dom"]),
        mesh=mesh,
        in_specs=(
            P(None, None, GRP_DOM), P(), P(), P(),
            P(None, None, None, GRP_DOM), P(None, None, None, GRP_DOM), P(None, None, None, GRP_DOM),
            P(None, GRP_DOM), P(None, GRP_DOM), P(GRP_DOM), P(GRP_DOM, None), P(GRP_DOM, None, None),
            P(GRP_DOM), P(GRP_DOM), P(None, GRP_DOM),
        ),
        out_specs=(P(None, None, GRP_DOM), P("grp", None), P(None, None, GRP_DOM)),
        check_vma=False,
    )
```

profile of v0, /device:TPU:24, one launch (start us, length us, event | category | flops | bytes accessed | tf_op | source)
XLA Modules:
  0.0 130.4 jit_solution(9617542235038323857)
XLA Ops:
  1.3 0.5 broadcast.41
  1.8 1.3 %reduce.3 = s32[8]{0:T(128)S(1)} reduce(s32[1,8]{1,0:T(1,128)} %param.25, s32[]{:T(128)} %broadcast.41), dimensions={0}, to_apply=%param.25.reduce_sub_computation.3 | reduce | bytes 68 | tf_op args[10]
  3.1 0.1 lt.54
  3.2 0.7 pad_bitcast_fusion
  3.9 0.1 lt.56
  4.0 0.1 lt.57
  4.0 0.1 lt.58
  4.1 0.8 squeeze.7
  4.9 0.6 compare_convert_fusion.live_ref
  5.5 0.7 pad.13
  6.2 0.7 concatenate.21
  6.9 0.6 add_convert_fusion.number_ref
  7.5 0.1 reshape.121
  7.6 0.7 broadcast_in_dim.10
  8.3 0.1 pad_maximum_fusion
  8.4 0.6 copy.22
  9.0 0.8 broadcast_multiply_fusion
  9.8 0.6 broadcast_in_dim.7.weight_ref
  10.4 114.9 %shard_map.166 = (f32[9,56,640]{2,1,0:T(8,128)}, f32[8,128]{1,0:T(8,128)}, f32[32,128]{1,0:T(8,128)}) custom-call(f32[9,56,640]{2,1,0:T(8,128)} %bitcast.19, f32[3,56,56]{2,1,0:T(8,128)} %stiff_ref.1, f32[4,56,56]{2,1,0:T(8,128)} %flux_ref.1, f32[4,56,56]{2,1,0:T(8,128)} %fluxr_ref.1, f32[9,9,3,640]{3,2,1,0:T(4,128)} %bitcast.21, f32[9,9,4,640]{3,2,1,0:T(4,128)} %bitcast.22, ...), custom_call_target="tpu_custom_call" | custom-call | tf_op jit(solution)/shard_map/pallas_call | solution.py:421
  125.4 1.3 slice_multiply_fusion
  126.6 0.7 reshape.123
  127.3 0.6 copy.19
  128.0 2.4 %copy.25 = f32[56,9,640]{2,0,1:T(8,128)} copy(f32[56,9,640]{2,0,1:T(8,128)} %bitcast.20) | data formatting | bytes 2580480
  (3 shorter events, 0.0 us)
where the time goes:
time: 131 us; the launch traced here: 130 us
  Pallas kernels  115 us (88%)
  local copies, waits for them, and re-layouts  9.49 us (7%)
  other arithmetic  4.68 us (4%)
    pallas_call x1, Pallas kernels, run(): pl.pallas_call(make_kernel(groups, places, elems, cap), out_shape=(jax.Sh...  115 us
    unnamed x4, local copies, waits for them, and re-layouts  4.19 us

commit v1 on v0

--- a/solution.py
+++ b/solution.py
@@ -39,16 +39,27 @@
     receivers = 16
 
     def kernel(
-        state_ref, stiff_ref, flux_ref, fluxr_ref, star_ref, face_ref, facer_ref,
-        weight_ref, live_ref, number_ref, recw_ref,
+        count_ref, send_count_ref, rec_element_ref, rec_slot_ref,
+        state_ref, stiff_ref, flux_ref, fluxr_ref, star_hbm, face_hbm, facer_hbm,
+        energy_weight_ref, near_ref, send_ref, rec_weight_ref,
         x_ref, energy_ref, trace_ref,
+        star_ref, face_ref, facer_ref, weight_ref, live_ref, recw_ref, names_ref,
         y_ref, v_ref, part_ref, xt_ref, send_buf, halo_ref, hb_ref, own_ref, nb_ref, vr_ref,
-        pick_ref, pack_ref, af_ref, a_ref, rf_ref, ra_ref, rb_ref,
+        pick_ref, pack_ref, af_ref, a_ref, rf_ref, ra_ref,
         en_ref, rec_ref, table_ref, msg_ref, all_ref,
-        send_sem, recv_sem, last_send, last_recv,
+        send_sem, recv_sem, last_send, last_recv, load_sem,
     ):
         g = lax.axis_index("grp")
         d = lax.axis_index("dom")
+
+        loads = [
+            pltpu.make_async_copy(source, held, load_sem.at[i])
+            for i, (source, held) in enumerate(
+                [(star_hbm, star_ref), (face_hbm, face_ref), (facer_hbm, facer_ref)]
+            )
+        ]
+        for load in loads:
+            load.start()
 
         for t in range(STEPS):
             halo_ref[t, 2 * REACH * cap :, :] = jnp.zeros((2 * cap, CHUNKS * LANES), f32)
@@ -71,23 +82,37 @@
 
         for q in range(9):
             x_ref[q] = state_ref[q]
+        here = lax.broadcasted_iota(jnp.int32, (1, elems), 1)
+        live = jnp.clip((count_ref[0] - here).astype(f32), 0.0, 1.0)
+        live_ref[...] = live
+        for q in range(9):
+            weight_ref[q] = energy_weight_ref[q : q + 1, :] * live
 
         lane = lax.broadcasted_iota(jnp.int32, (LANES, LANES), 1).astype(f32)
 
-        def column(number):
-            return jnp.broadcast_to(number_ref[number], (LANES, LANES)).T
-
         def hot(names, tile):
-            return jnp.maximum(1.0 - jnp.abs(names - (lane + float(tile * LANES))), 0.0).astype(bf16)
-
-        def pack_rows(i, carry):
-            names = column(4 * blocks + i)
-            at = pl.ds(pl.multiple_of(i * LANES, LANES), LANES)
+            return jnp.maximum(1.0 - jnp.abs(names - (lane[: names.shape[0]] + float(tile * LANES))), 0.0).astype(bf16)
+
+        names_ref[...] = jnp.zeros_like(names_ref)
+        names_ref[0:slots, 0:cap] = send_ref[0].astype(f32)
+        turned = names_ref[...].T
+        order = lax.broadcasted_iota(jnp.int32, (cap, LANES), 0)
+        for slot in range(slots):
+            sends = jnp.clip((send_count_ref[0, slot] - order).astype(f32), 0.0, 1.0)
+            names = (jnp.broadcast_to(turned[:cap, slot : slot + 1], (cap, LANES)) + 1.0) * sends - 1.0
             for tile in range(blocks):
-                pack_ref[at, tile * LANES : (tile + 1) * LANES] = hot(names, tile)
-            return carry
-
-        lax.fori_loop(0, sent // LANES + 1, pack_rows, 0)
+                pack_ref[slot * cap : (slot + 1) * cap, tile * LANES : (tile + 1) * LANES] = hot(names, tile)
+
+        def listed(ref):
+            rows = lax.broadcasted_iota(jnp.int32, (receivers, LANES), 0)
+            total = jnp.zeros((receivers, LANES), f32)
+            for r in range(receivers):
+                total = total + jnp.where(rows == r, 1.0, 0.0) * ref[r].astype(f32)
+            return total
+
+        names = listed(rec_element_ref)
+        for tile in range(blocks):
+            pack_ref[sent : sent + receivers, tile * LANES : (tile + 1) * LANES] = hot(names, tile)
 
         def to_rows():
             def body(block, carry):
@@ -191,18 +216,27 @@
                         size = min(16, 56 - 16 * j)
                         rf_ref[pl.ds(112, 56), pl.ds(112, size)] = matrix[:, 16 * j : 16 * j + size]
                         hi, lo = split(rf_ref[...])
-                        ra_ref[f, j] = jnp.concatenate([hi, hi], axis=1)
-                        rb_ref[f, j] = jnp.concatenate([lo, lo], axis=1)
-
-                def face_rows(i, carry):
-                    names = column(i)
-                    f = i // blocks
-                    at = pl.ds(pl.multiple_of(i % blocks * LANES, LANES), LANES)
-                    for tile in range(blocks + sent // LANES):
-                        pick_ref[f, at, tile * LANES : (tile + 1) * LANES] = hot(names, tile)
+                        ra_ref[f, j, :ROWS_LHS] = jnp.concatenate([hi, hi], axis=1)
+                        ra_ref[f, j, ROWS_LHS:] = jnp.concatenate([lo, lo], axis=1)
+
+                def face_rows(block, carry):
+                    at = lane_block(block)
+                    for f in range(4):
+                        row = near_ref[f : f + 1, at].astype(f32)
+                        names = jnp.broadcast_to(row, (LANES, LANES)).T
+                        for tile in range(blocks + sent // LANES):
+                            pick_ref[f, at, tile * LANES : (tile + 1) * LANES] = hot(names, tile)
                     return carry
 
-                lax.fori_loop(0, 4 * blocks, face_rows, 0)
+                lax.fori_loop(0, blocks, face_rows, 0)
+                for j in range(CHUNKS):
+                    size = min(16, 56 - 16 * j)
+                    recw_ref[:, j * LANES : (j + 1) * LANES] = jnp.zeros((receivers, LANES), f32)
+                    recw_ref[:, j * LANES : j * LANES + 56] = rec_weight_ref[...]
+                    recw_ref[:, j * LANES + 56 : j * LANES + 112] = rec_weight_ref[...]
+                    recw_ref[:, j * LANES + 112 : j * LANES + 112 + size] = rec_weight_ref[:, 16 * j : 16 * j + size]
+                for load in loads:
+                    load.wait()
 
             @pl.when(t > 0)
             def _():
@@ -275,7 +309,7 @@
                     nb_ref[...] = own_ref[f, j] + far
                     near = nb_ref[...]
                     both = lax.dot_general(ra_ref[f, j], near, NT, preferred_element_type=f32)
-                    both = both + lax.dot_general(rb_ref[f, j], near, NT, preferred_element_type=f32)
+                    both = both[:ROWS_LHS] + both[ROWS_LHS:]
                     vr_ref[f, 2 * j] = both[0:56]
                     vr_ref[f, 2 * j + 1] = both[56:112]
                     if j == 0:
@@ -290,7 +324,7 @@
                 block = number // 3
                 first = (number % 3) * 3
                 at = lane_block(block)
-                live = live_ref[0, :, at]
+                live = live_ref[:, at]
                 total = [part_ref[first + i, :, at] for i in range(3)]
                 for f in range(4):
                     for q in range(9):
@@ -328,7 +362,7 @@
 
         row = lax.broadcasted_iota(jnp.int32, (receivers, LANES), 0)
         col = lax.broadcasted_iota(jnp.int32, (receivers, LANES), 1)
-        rows = column(4 * blocks + sent // LANES + 1)[:receivers]
+        rows = listed(rec_slot_ref)
         sums = jnp.sum(en_ref[...], axis=1, keepdims=True)
         table = table_ref[...] + jnp.where(col == 27, rows, 0.0)
         for t in range(STEPS):
@@ -370,18 +404,21 @@
         lax.fori_loop(1, places, end_last, 0)
 
         arrived = all_ref[...].reshape(places * half, LANES)
-        energy_ref[...] = jnp.broadcast_to(jnp.sum(arrived, axis=0, keepdims=True), energy_ref.shape)
+        summed = jnp.sum(arrived, axis=0, keepdims=True)
+        energy_ref[...] = summed[:, 28 : 28 + STEPS] * (0.5 / float(places * elems * 56 * 9))
         mine = lax.broadcasted_iota(jnp.int32, (places * half, LANES), 1).astype(f32)
         mine = mine + (d * receivers).astype(f32)
         keep = lax.broadcasted_iota(jnp.int32, (places * half, LANES), 1) < receivers
-        result = jnp.zeros(trace_ref.shape, f32)
+        result = jnp.zeros((32, LANES), f32)
         for part in range(2):
             names = jnp.broadcast_to(arrived[:, 64 * part + 27 : 64 * part + 28], (places * half, LANES))
             chosen = jnp.maximum(1.0 - jnp.abs(names - mine), 0.0)
             chosen = jnp.where(keep, chosen, 0.0)
             picked = lax.dot_general(arrived, chosen, TN, precision=highest, preferred_element_type=f32)
             result = result + picked[64 * part : 64 * part + 32]
-        trace_ref[...] = result
+        for t in range(STEPS):
+            for q in range(9):
+                trace_ref[q, t : t + 1, :] = result[9 * t + q : 9 * t + q + 1, :receivers]
 
     return kernel
 
@@ -396,38 +433,28 @@
         slots, cap = send_element.shape[1:]
         sent = slots * cap
         receivers = receiver_slot.shape[0]
-        turned = receiver_weight.T
-        tail = jnp.pad(turned, ((0, 0), (0, 8))).reshape(receivers, CHUNKS, 16)
-        pair = jnp.broadcast_to(turned[:, None, :], (receivers, CHUNKS, basis))
-        recw = jnp.concatenate([pair, pair, tail], axis=2).reshape(receivers, CHUNKS * LANES)
-        live = (jnp.arange(elems) < element_count[0]).astype(f32)
-        weight = (energy_weight * live[None])[:, None, :]
-        filled = jnp.arange(cap)[None, :] < send_count[0][:, None]
-        wanted = jnp.where(filled, send_element[0], -1)
-        fill = LANES - receivers
-        numbers = jnp.concatenate(
-            [
-                face_neighbour.reshape(-1, LANES),
-                wanted.reshape(-1, LANES),
-                jnp.pad(receiver_element, (0, fill), constant_values=-1)[None],
-                jnp.pad(receiver_slot, (0, fill), constant_values=-1)[None],
-            ],
-            axis=0,
-        ).astype(f32)[:, None, :]
-
         vmem = pl.BlockSpec(memory_space=pltpu.VMEM)
+        smem = pl.BlockSpec(memory_space=pltpu.SMEM)
+        hbm = pl.BlockSpec(memory_space=pl.ANY)
         wide = CHUNKS * LANES
         faces = 4
-        state, energy, table = pl.pallas_call(
+        state, energy, traces = pl.pallas_call(
             make_kernel(groups, places, elems, cap),
             out_shape=(
                 jax.ShapeDtypeStruct((quantities, basis, elems), f32),
-                jax.ShapeDtypeStruct((8, LANES), f32),
-                jax.ShapeDtypeStruct((32, LANES), f32),
+                jax.ShapeDtypeStruct((1, STEPS), f32),
+                jax.ShapeDtypeStruct((quantities, STEPS, receivers), f32),
             ),
-            in_specs=[vmem] * 11,
+            in_specs=[smem] * 4 + [vmem] * 4 + [hbm] * 3 + [vmem] * 4,
             out_specs=(vmem, vmem, vmem),
             scratch_shapes=[
+                pltpu.VMEM((9, 9, 3, elems), f32),
+                pltpu.VMEM((9, 9, faces, elems), f32),
+                pltpu.VMEM((9, 9, faces, elems), f32),
+                pltpu.VMEM((9, 1, elems), f32),
+                pltpu.VMEM((1, elems), f32),
+                pltpu.VMEM((receivers, wide), f32),
+                pltpu.VMEM((LANES, LANES), f32),
                 pltpu.VMEM((256, elems), bf16),
                 pltpu.VMEM((9, 400, elems), f32),
                 pltpu.VMEM((9, 56, elems), f32),
@@ -443,8 +470,7 @@
                 pltpu.VMEM((400, 256), f32),
                 pltpu.VMEM((400, 256), bf16),
                 pltpu.VMEM((ROWS_LHS, LANES), f32),
-                pltpu.VMEM((faces, CHUNKS, ROWS_LHS, 2 * LANES), bf16),
-                pltpu.VMEM((faces, CHUNKS, ROWS_LHS, 2 * LANES), bf16),
+                pltpu.VMEM((faces, CHUNKS, 2 * ROWS_LHS, 2 * LANES), bf16),
                 pltpu.VMEM((8, LANES), f32),
                 pltpu.VMEM((receivers, wide), f32),
                 pltpu.VMEM((receivers, LANES), f32),
@@ -454,19 +480,19 @@
                 pltpu.SemaphoreType.DMA((STEPS, slots)),
                 pltpu.SemaphoreType.DMA((places,)),
                 pltpu.SemaphoreType.DMA((places,)),
+                pltpu.SemaphoreType.DMA((3,)),
             ],
             compiler_params=pltpu.CompilerParams(
                 collective_id=0, has_side_effects=True, vmem_limit_bytes=60 * 1024 * 1024
             ),
         )(
+            element_count, send_count, receiver_element, receiver_slot,
             element_state.transpose(1, 0, 2), stiffness, flux_local, flux_remote,
             star_matrix.transpose(1, 2, 0, 3), face_local.transpose(1, 2, 0, 3),
             face_remote.transpose(1, 2, 0, 3),
-            weight, live[None, None], numbers, recw,
+            energy_weight, face_neighbour, send_element, receiver_weight.T,
         )
-        total = energy[:1, 28 : 28 + STEPS] * 0.5 / float(places * elems * basis * quantities)
-        traces = table[: STEPS * quantities, :receivers].reshape(STEPS, quantities, receivers)
-        return state.transpose(1, 0, 2), total, traces
+        return state.transpose(1, 0, 2), energy, traces.transpose(1, 0, 2)
 
     return run
 

time: 131 us -> 116 us (0.89)
  local copies, waits for them, and re-layouts: 9.49 us -> 3.57 us
  other arithmetic: 4.68 us -> 0 us
  Pallas kernels: 115 us -> 111 us
    pallas_call x1, Pallas kernels: 115 us -> 111 us  [run(): pl.pallas_call(make_kernel(groups, places, elems, cap), out_shape=(jax.Sh...]
    concatenate x2 -> x0, local copies, waits for them, and re-layouts: 1.39 us -> none  [run(): jnp.concatenate([face_neighbour.reshape(-1, LANES), wanted.reshape(-1, LA...]
    broadcast_in_dim x2 -> x0, local copies, waits for them, and re-layouts: 1.32 us -> none  [the longest x1 0.71 us: run(): pair = jnp.broadcast_to(turned[:, None, :], (receivers, CHUNKS, basis))]
    unnamed x1 -> x0, other arithmetic: 1.32 us -> none
    unnamed x4 -> x7, local copies, waits for them, and re-layouts: 4.19 us -> 3.57 us
where the time goes in v1:
time: 116 us; the launch traced here: 115 us
  Pallas kernels  111 us (96%)
  local copies, waits for them, and re-layouts  3.57 us (3%)
  between operations  1.31 us (1%)
    pallas_call x1, Pallas kernels, run(): pl.pallas_call(make_kernel(groups, places, elems, cap), out_shape=(jax.Sh...  111 us
    unnamed x7, local copies, waits for them, and re-layouts  3.57 us

profile of v1, /device:TPU:24, one launch (start us, length us, event | category | flops | bytes accessed | tf_op | source)
XLA Modules:
  0.0 115.4 jit_solution(11770375495792873914)
XLA Ops:
  1.3 110.5 %shard_map.166 = (f32[9,56,640]{2,1,0:T(8,128)}, f32[1,3]{1,0:T(1,128)}, f32[9,3,16]{2,1,0:T(4,128)}) custom-call(s32[1]{0:T(128)S(6)} %copy.21.count_ref, s32[1,8]{1,0:T(1,128)} %send_count_ref.1, s32[16]{0:T(128)} %rec_element_ref.1, s32[16]{0:T(128)} %rec_slot_ref.1, f32[9,56,640]{2,1,0:T(8,128)} %bitcast.8, f32[3,56,56]{2,1,0:T(8,128)} %stiff_ref.1, ...), custom_call_target="tpu_custom_call" | custom-call | tf_op jit(solution)/shard_map/pallas_call | solution.py:441
  111.8 0.0 copy-start.1
  111.8 0.0 copy-start
  111.8 2.4 %copy.22 = f32[56,9,640]{2,0,1:T(8,128)} copy(f32[56,9,640]{2,0,1:T(8,128)} %bitcast.7) | data formatting | bytes 2580480
  114.3 0.0 copy-done.1
  114.3 0.5 copy.23
  114.8 0.0 copy-done
  114.8 0.6 copy.24
Async XLA Ops:
  111.8 2.5 %copy-start.1 = (f32[1,3]{1,0:T(1,128)S(1)}, f32[1,3]{1,0:T(1,128)}, u32[]{:S(2)}) copy-start(f32[1,3]{1,0:T(1,128)} %get-tuple-element.13) | copy-start | bytes 40
  111.8 3.0 %copy-start = (f32[9,3,16]{2,1,0:T(4,128)S(1)}, f32[9,3,16]{2,1,0:T(4,128)}, u32[]{:S(2)}) copy-start(f32[9,3,16]{2,1,0:T(4,128)} %get-tuple-element.8) | copy-start | bytes 5188

commit v2 on v1

--- a/solution.py
+++ b/solution.py
@@ -44,7 +44,7 @@
         energy_weight_ref, near_ref, send_ref, rec_weight_ref,
         x_ref, energy_ref, trace_ref,
         star_ref, face_ref, facer_ref, weight_ref, live_ref, recw_ref, names_ref,
-        y_ref, v_ref, part_ref, xt_ref, send_buf, halo_ref, hb_ref, own_ref, nb_ref, vr_ref,
+        y_ref, v_ref, part_ref, xt_ref, send_buf, halo_ref, hb_ref, own_ref, nb_ref, vra_ref, vrb_ref,
         pick_ref, pack_ref, af_ref, a_ref, rf_ref, ra_ref,
         en_ref, rec_ref, table_ref, msg_ref, all_ref,
         send_sem, recv_sem, last_send, last_recv, load_sem,
@@ -268,20 +268,19 @@
                             total[i] = total[i] + maps[first + i, q, pl.ds(n, 1), at] * term
                 for i in range(3):
                     part_ref[first + i, :, at] = total[i]
+                own(number)
                 return carry
 
+            def own(unit):
+                f, j = unit // CHUNKS, unit % CHUNKS
+                pair = pl.ds(pl.multiple_of(j * 2 * LANES, 2 * LANES), 2 * LANES)
+                own_ref[f, j] = jnp.dot(
+                    pick_ref[f, :, :elems], xt_ref[:, pair], preferred_element_type=f32
+                ).astype(bf16)
+
             lax.fori_loop(0, blocks * 3, local_map, 0)
-
-            def own(f, carry):
-                for j in range(CHUNKS):
-                    own_ref[f, j] = jnp.dot(
-                        pick_ref[f, :, :elems],
-                        xt_ref[:, 2 * j * LANES : (2 * j + 2) * LANES],
-                        preferred_element_type=f32,
-                    ).astype(bf16)
-                return carry
-
-            lax.fori_loop(0, 4, own, 0)
+            for unit in range(blocks * 3, 4 * CHUNKS):
+                own(unit)
 
             for slot in range(2 * REACH):
                 moves[slot].wait_recv()
@@ -299,26 +298,43 @@
                 hb_ref[:, 2 * j * LANES : (2 * j + 1) * LANES] = hi
                 hb_ref[:, (2 * j + 1) * LANES : (2 * j + 2) * LANES] = lo
 
-            def remote(f, carry):
-                for j in range(CHUNKS):
-                    far = jnp.dot(
-                        pick_ref[f, :, elems:],
-                        hb_ref[:, 2 * j * LANES : (2 * j + 2) * LANES],
-                        preferred_element_type=f32,
-                    ).astype(bf16)
-                    nb_ref[...] = own_ref[f, j] + far
-                    near = nb_ref[...]
-                    both = lax.dot_general(ra_ref[f, j], near, NT, preferred_element_type=f32)
-                    both = both[:ROWS_LHS] + both[ROWS_LHS:]
-                    vr_ref[f, 2 * j] = both[0:56]
-                    vr_ref[f, 2 * j + 1] = both[56:112]
-                    if j == 0:
-                        vr_ref[f, 8] = both[112:168]
-                    else:
-                        vr_ref[f, 8] += both[112:168]
-                return carry
-
-            lax.fori_loop(0, 4, remote, 0)
+            def far_unit(f, j, held):
+                far = jnp.dot(
+                    pick_ref[f, :, elems:],
+                    hb_ref[:, 2 * j * LANES : (2 * j + 2) * LANES],
+                    preferred_element_type=f32,
+                ).astype(bf16)
+                nb_ref[...] = own_ref[f, j] + far
+                both = lax.dot_general(ra_ref[f, j], nb_ref[...], NT, preferred_element_type=f32)
+                both = both[:ROWS_LHS] + both[ROWS_LHS:]
+                held[2 * j] = both[0:56]
+                held[2 * j + 1] = both[56:112]
+                if j == 0:
+                    held[8] = both[112:168]
+                else:
+                    held[8] += both[112:168]
+
+            def face_map(f, held, block, first):
+                at = pl.ds(block * LANES, LANES)
+                total = [part_ref[first + i, :, at] for i in range(3)]
+                for q in range(9):
+                    term = held[q, :, at]
+                    for i in range(3):
+                        total[i] = total[i] + facer_ref[first + i, q, f : f + 1, at] * term
+                for i in range(3):
+                    part_ref[first + i, :, at] = total[i]
+
+            held = [vra_ref, vrb_ref]
+            units = [(block, 3 * i) for block in range(blocks) for i in range(3)]
+            for f in range(4):
+
+                @pl.when(t < STEPS + f)
+                def _():
+                    for j in range(CHUNKS):
+                        far_unit(f, j, held[f % 2])
+                        if f > 0:
+                            for block, first in units[j::CHUNKS]:
+                                face_map(f - 1, held[(f - 1) % 2], block, first)
 
             def remote_map(number, energy):
                 block = number // 3
@@ -326,11 +342,10 @@
                 at = lane_block(block)
                 live = live_ref[:, at]
                 total = [part_ref[first + i, :, at] for i in range(3)]
-                for f in range(4):
-                    for q in range(9):
-                        term = vr_ref[f, q, :, at]
-                        for i in range(3):
-                            total[i] = total[i] + facer_ref[first + i, q, pl.ds(f, 1), at] * term
+                for q in range(9):
+                    term = vrb_ref[q, :, at]
+                    for i in range(3):
+                        total[i] = total[i] + facer_ref[first + i, q, pl.ds(3, 1), at] * term
                 for i in range(3):
                     new = x_ref[first + i, :, at] + live * total[i]
                     x_ref[first + i, :, at] = new
@@ -464,7 +479,8 @@
                 pltpu.VMEM((sent, 2 * wide), bf16),
                 pltpu.VMEM((faces, CHUNKS, elems, 2 * LANES), bf16),
                 pltpu.VMEM((elems, 2 * LANES), bf16),
-                pltpu.VMEM((faces, 9, 56, elems), f32),
+                pltpu.VMEM((9, 56, elems), f32),
+                pltpu.VMEM((9, 56, elems), f32),
                 pltpu.VMEM((faces, elems, elems + sent), bf16),
                 pltpu.VMEM((sent + LANES, elems), bf16),
                 pltpu.VMEM((400, 256), f32),

time: 116 us -> 108 us (0.931)
  Pallas kernels: 111 us -> 103 us
    pallas_call x1, Pallas kernels: 111 us -> 103 us  [run(): pl.pallas_call(make_kernel(groups, places, elems, cap), out_shape=(jax.Sh...]
where the time goes in v2:
time: 108 us
  Pallas kernels  103 us (95%)
  local copies, waits for them, and re-layouts  3.57 us (3%)
  between operations  1.31 us (1%)
    pallas_call x1, Pallas kernels, run(): pl.pallas_call(make_kernel(groups, places, elems, cap), out_shape=(jax.Sh...  103 us
    unnamed x7, local copies, waits for them, and re-layouts  3.57 us

profile of v2, /device:TPU:24, one launch (start us, length us, event | category | flops | bytes accessed | tf_op | source)
XLA Modules:
  0.0 108.1 jit_solution(14516640950775423484)
XLA Ops:
  1.3 103.2 %shard_map.166 = (f32[9,56,640]{2,1,0:T(8,128)}, f32[1,3]{1,0:T(1,128)}, f32[9,3,16]{2,1,0:T(4,128)}) custom-call(s32[1]{0:T(128)S(6)} %copy.21.count_ref, s32[1,8]{1,0:T(1,128)} %send_count_ref.1, s32[16]{0:T(128)} %rec_element_ref.1, s32[16]{0:T(128)} %rec_slot_ref.1, f32[9,56,640]{2,1,0:T(8,128)} %bitcast.8, f32[3,56,56]{2,1,0:T(8,128)} %stiff_ref.1, ...), custom_call_target="tpu_custom_call" | custom-call | tf_op jit(solution)/shard_map/pallas_call | solution.py:456
  104.5 0.0 copy-start.1
  104.5 0.0 copy-start
  104.5 2.4 %copy.22 = f32[56,9,640]{2,0,1:T(8,128)} copy(f32[56,9,640]{2,0,1:T(8,128)} %bitcast.7) | data formatting | bytes 2580480
  107.0 0.0 copy-done.1
  107.0 0.5 copy.23
  107.5 0.0 copy-done
  107.5 0.6 copy.24
Async XLA Ops:
  104.5 2.5 %copy-start.1 = (f32[1,3]{1,0:T(1,128)S(1)}, f32[1,3]{1,0:T(1,128)}, u32[]{:S(2)}) copy-start(f32[1,3]{1,0:T(1,128)} %get-tuple-element.13) | copy-start | bytes 40
  104.5 3.0 %copy-start = (f32[9,3,16]{2,1,0:T(4,128)S(1)}, f32[9,3,16]{2,1,0:T(4,128)}, u32[]{:S(2)}) copy-start(f32[9,3,16]{2,1,0:T(4,128)} %get-tuple-element.8) | copy-start | bytes 5188

commit v3 on v2

--- a/solution.py
+++ b/solution.py
@@ -90,8 +90,9 @@
 
         lane = lax.broadcasted_iota(jnp.int32, (LANES, LANES), 1).astype(f32)
 
-        def hot(names, tile):
-            return jnp.maximum(1.0 - jnp.abs(names - (lane[: names.shape[0]] + float(tile * LANES))), 0.0).astype(bf16)
+        def hot(away, tile):
+            step = (away - float(tile * LANES)).astype(bf16)
+            return jnp.maximum(1.0 - step * step, 0.0)
 
         names_ref[...] = jnp.zeros_like(names_ref)
         names_ref[0:slots, 0:cap] = send_ref[0].astype(f32)
@@ -100,8 +101,9 @@
         for slot in range(slots):
             sends = jnp.clip((send_count_ref[0, slot] - order).astype(f32), 0.0, 1.0)
             names = (jnp.broadcast_to(turned[:cap, slot : slot + 1], (cap, LANES)) + 1.0) * sends - 1.0
+            away = names - lane[:cap]
             for tile in range(blocks):
-                pack_ref[slot * cap : (slot + 1) * cap, tile * LANES : (tile + 1) * LANES] = hot(names, tile)
+                pack_ref[slot * cap : (slot + 1) * cap, tile * LANES : (tile + 1) * LANES] = hot(away, tile)
 
         def listed(ref):
             rows = lax.broadcasted_iota(jnp.int32, (receivers, LANES), 0)
@@ -110,9 +112,9 @@
                 total = total + jnp.where(rows == r, 1.0, 0.0) * ref[r].astype(f32)
             return total
 
-        names = listed(rec_element_ref)
+        away = listed(rec_element_ref) - lane[:receivers]
         for tile in range(blocks):
-            pack_ref[sent : sent + receivers, tile * LANES : (tile + 1) * LANES] = hot(names, tile)
+            pack_ref[sent : sent + receivers, tile * LANES : (tile + 1) * LANES] = hot(away, tile)
 
         def to_rows():
             def body(block, carry):
@@ -223,9 +225,9 @@
                     at = lane_block(block)
                     for f in range(4):
                         row = near_ref[f : f + 1, at].astype(f32)
-                        names = jnp.broadcast_to(row, (LANES, LANES)).T
+                        away = jnp.broadcast_to(row, (LANES, LANES)).T - lane
                         for tile in range(blocks + sent // LANES):
-                            pick_ref[f, at, tile * LANES : (tile + 1) * LANES] = hot(names, tile)
+                            pick_ref[f, at, tile * LANES : (tile + 1) * LANES] = hot(away, tile)
                     return carry
 
                 lax.fori_loop(0, blocks, face_rows, 0)

time: 108 us -> 108 us (level)
  no operation moved by 1% of the time
where the time goes in v3:
time: 108 us
  Pallas kernels  103 us (95%)
  local copies, waits for them, and re-layouts  3.57 us (3%)
  between operations  1.31 us (1%)
    pallas_call x1, Pallas kernels, run(): pl.pallas_call(make_kernel(groups, places, elems, cap), out_shape=(jax.Sh...  103 us
    unnamed x7, local copies, waits for them, and re-layouts  3.57 us

profile of v3, /device:TPU:24, one launch (start us, length us, event | category | flops | bytes accessed | tf_op | source)
XLA Modules:
  0.0 107.6 jit_solution(17934660847543913048)
XLA Ops:
  1.3 102.7 %shard_map.166 = (f32[9,56,640]{2,1,0:T(8,128)}, f32[1,3]{1,0:T(1,128)}, f32[9,3,16]{2,1,0:T(4,128)}) custom-call(s32[1]{0:T(128)S(6)} %copy.21.count_ref, s32[1,8]{1,0:T(1,128)} %send_count_ref.1, s32[16]{0:T(128)} %rec_element_ref.1, s32[16]{0:T(128)} %rec_slot_ref.1, f32[9,56,640]{2,1,0:T(8,128)} %bitcast.8, f32[3,56,56]{2,1,0:T(8,128)} %stiff_ref.1, ...), custom_call_target="tpu_custom_call" | custom-call | tf_op jit(solution)/shard_map/pallas_call | solution.py:458
  104.0 0.0 copy-start.1
  104.0 0.0 copy-start
  104.0 2.4 %copy.22 = f32[56,9,640]{2,0,1:T(8,128)} copy(f32[56,9,640]{2,0,1:T(8,128)} %bitcast.7) | data formatting | bytes 2580480
  106.5 0.0 copy-done.1
  106.5 0.5 copy.23
  107.0 0.0 copy-done
  107.0 0.6 copy.24
Async XLA Ops:
  104.0 2.5 %copy-start.1 = (f32[1,3]{1,0:T(1,128)S(1)}, f32[1,3]{1,0:T(1,128)}, u32[]{:S(2)}) copy-start(f32[1,3]{1,0:T(1,128)} %get-tuple-element.13) | copy-start | bytes 40
  104.0 3.0 %copy-start = (f32[9,3,16]{2,1,0:T(4,128)S(1)}, f32[9,3,16]{2,1,0:T(4,128)}, u32[]{:S(2)}) copy-start(f32[9,3,16]{2,1,0:T(4,128)} %get-tuple-element.8) | copy-start | bytes 5188
